TPU v7x, 512 devices: a whole 4x8x8 slice. The times are simulated.
512 devices in a mesh: cls: 32 (over z, x_hi, core), dp: 16 (over y, x_lo).
Axes of the slice: x: 4 (x_hi: 2, x_lo: 2; x = x_hi * 2 + x_lo), y: 8, z: 8, core: 2. Of those that a mesh axis runs over, the one named last changes fastest.
Arguments:
- hidden: bfloat16 [320, 3072], P('dp'), may hold values from -7 to 7
- weight: bfloat16 [196608, 3072], P(('cls', 'dp')), may hold values from -8 to 8
- labels: int32 [320], replicated, may hold values from 0 to 196607
- cotangent: float32 [320], replicated, may hold values from -4 to 4
Outputs:
- token_loss: float32 [320], P('dp')
- weight_grad: bfloat16 [196608, 3072], P(('cls', 'dp'))
- hidden_grad: bfloat16 [320, 3072], P('dp', 'cls')
All inputs are finite; a program needn't handle non-finite values.
Results may differ from a plain program's by a relative error of at most 0.0049.
Values may be sent and summed in bfloat16 or wider, within the bound.
A program may use at most 64 MiB of HBM per device.

v0:
```python
import jax
import jax.numpy as jnp
from jax import lax
from jax.sharding import Mesh
from jax.sharding import PartitionSpec as P

CLS = ("cls_0", "cls_1", "cls_2")
DP = ("dp_0", "dp_1")
CLS_DP = ("cls_0", "cls_1", "cls_2", "dp_0", "dp_1")


def joined_along(pieces, dim):
    pieces = jnp.moveaxis(pieces, 0, dim)
    lengths = pieces.shape
    return pieces.reshape(*lengths[:dim], lengths[dim] * lengths[dim + 1], *lengths[dim + 2 :])


def copy_for_each(shard, axis):
    peers = lax.axis_size(axis)
    return lax.all_to_all(
        jnp.broadcast_to(shard[None], (peers, *shard.shape)), axis, 0, 0, tiled=True
    )


def gather_directly(shard, axis, dim):
    return joined_along(copy_for_each(shard, axis), dim)


def collected_together(shard, axis):
    leaves = jax.tree.leaves(shard)
    sequence = sorted(range(len(leaves)), key=lambda k: -leaves[k].size)
    width = (1, *leaves[sequence[0]].shape)[-1]
    lines = [
        jnp.pad(leaves[k].reshape(-1), (0, -leaves[k].size % width)).reshape(-1, width)
        for k in sequence
    ]
    both, at, found = (lax.all_gather(jnp.concatenate(lines), axis), 0, {})
    for k, line in zip(sequence, lines):
        piece = both[:, at : at + len(line)].reshape(len(both), -1)
        found[k] = piece[:, : leaves[k].size].reshape(-1, *leaves[k].shape)
        at += len(line)
    numbers = iter(range(len(leaves)))
    return jax.tree.map(lambda _: found[next(numbers)], shard)


def combined_by_axis(shard, axes, combine):
    for axis in axes:
        pieces = collected_together(shard, axis)
        shard = jax.tree.map(lambda part: part[0], pieces)
        for k in range(1, lax.axis_size(axis)):
            shard = combine(shard, jax.tree.map(lambda part: part[k], pieces))
    return shard


def summed_rows_2(so_far, axes):
    for axis in axes:
        so_far = lax.psum_scatter(so_far, axis, scatter_dimension=0, tiled=True)
    return so_far


def cut_along(shard, dim, peers):
    lengths = shard.shape
    pieces = shard.reshape(*lengths[:dim], peers, lengths[dim] // peers, *lengths[dim + 1 :])
    return jnp.moveaxis(pieces, dim, 0)


def summed_on_arrival(shard, axis, dim):
    pieces = cut_along(shard, dim, lax.axis_size(axis))
    arrived = lax.all_to_all(pieces, axis, split_axis=0, concat_axis=0, tiled=True)
    return arrived.sum(axis=0)


def combine_parts(earlier, later):
    new_peak = jnp.maximum(earlier[0], later[0])
    new_total = earlier[1] * jnp.exp(earlier[0] - new_peak) + later[1] * jnp.exp(
        later[0] - new_peak
    )
    return (new_peak, new_total, earlier[2] + later[2])


def body(hidden, weight, labels, cotangent):
    tok_count = hidden.shape[0]
    row_count = weight.shape[0]
    offset = (lax.axis_index(CLS) * lax.axis_size(DP) + lax.axis_index(DP)) * row_count
    gathered = gather_directly(hidden, DP, 0)
    logits = lax.dot_general(
        gathered, weight, (((1,), (1,)), ((), ())), preferred_element_type=jnp.float32
    )
    columns = offset + lax.broadcasted_iota(jnp.int32, logits.shape, 1)
    chosen = columns == labels[:, None]
    picked_here = jnp.sum(jnp.where(chosen, logits, jnp.zeros_like(logits)), axis=1)
    local_peak = jnp.max(logits, axis=1)
    local_total = jnp.sum(jnp.exp(logits - local_peak[:, None]), axis=1)
    peak_all, total_all, picked_all = combined_by_axis(
        (local_peak, local_total, picked_here), CLS_DP, combine_parts
    )
    loss_all = peak_all + jnp.log(total_all) - picked_all
    token_loss = lax.dynamic_slice_in_dim(loss_all, lax.axis_index(DP) * tok_count, tok_count)
    softmax_vals = jnp.exp(logits - peak_all[:, None]) / total_all[:, None]
    grad_logits = (cotangent[:, None] * (softmax_vals - chosen.astype(jnp.float32))).astype(
        jnp.bfloat16
    )
    weight_grad = lax.dot_general(
        grad_logits, gathered, (((0,), (0,)), ((), ())), preferred_element_type=jnp.float32
    ).astype(jnp.bfloat16)
    summed_rows = summed_rows_2(
        jnp.dot(grad_logits, weight, preferred_element_type=jnp.float32), DP
    )
    hidden_grad = summed_on_arrival(summed_rows, CLS, 1).astype(jnp.bfloat16)
    return (token_loss, weight_grad, hidden_grad)


def solution(mesh):
    torus = Mesh(mesh.devices.reshape(8, 2, 2, 8, 2), ("cls_0", "cls_1", "cls_2", "dp_0", "dp_1"))
    in_specs = (P(DP, None), P(CLS_DP, None), P(), P())
    out_specs = (P(DP), P(CLS_DP, None), P(DP, CLS))
    return jax.shard_map(body, mesh=torus, in_specs=in_specs, out_specs=out_specs, check_vma=False)
```

profile of v0, /device:TPU:1, one launch (start us, length us, event | category | flops | bytes accessed | tf_op | source)
XLA Modules:
  0.0 258.2 jit_solution(18134510374476593028)
XLA Ops:
  7.2 0.0 copy-start
  7.2 2.7 %broadcast_in_dim.4 = bf16[16,20,3072]{2,1,0:T(8,128)(2,1)} broadcast(bf16[20,3072]{1,0:T(8,128)(2,1)} %param.4), dimensions={1,2} | broadcast | bytes 2088960 | tf_op jit(solution)/shard_map/broadcast_in_dim | solution.py:21
  9.9 8.7 %all-to-all-start = ((bf16[16,20,3072]{2,1,0:T(8,128)(2,1)}), bf16[16,20,3072]{2,1,0:T(8,128)(2,1)}, u32[]{:S(2)}, u32[]{:S(2)}) async-start(bf16[16,20,3072]{2,1,0:T(8,128)(2,1)} %broadcast_in_dim.4), calls=%async_computation | async-start | bytes 4718592 | tf_op jit(solution)/shard_map/all_to_all | solution.py:20
  18.6 0.0 reduce-scatter.4.cloned.1.call-start
  18.7 54.3 %all-to-all-done = bf16[16,20,3072]{2,1,0:T(8,128)(2,1)} async-done(((bf16[16,20,3072]{2,1,0:T(8,128)(2,1)}), bf16[16,20,3072]{2,1,0:T(8,128)(2,1)}, u32[]{:S(2)}, u32[]{:S(2)}) %all-to-all-start) | async-done | bytes 1966112 | tf_op jit(solution)/shard_map/all_to_all | solution.py:20
  73.0 4.0 %reshape.1283 = bf16[320,3072]{1,0:T(8,128)(2,1)} reshape(bf16[16,20,3072]{2,1,0:T(8,128)(2,1)} %all-to-all-done) | data formatting | bytes 3932160 | tf_op jit(solution)/shard_map/reshape | solution.py:15
  77.0 0.0 copy-done
  77.0 2.9 %fusion.81 = (f32[320]{0:T(512)S(1)}, f32[320,384]{1,0:T(8,128)S(1)}) fusion(bf16[320,3072]{1,0:T(8,128)(2,1)} %reshape.1283, bf16[384,3072]{1,0:T(8,128)(2,1)S(1)} %copy-done), kind=kOutput, calls=%fused_computation.149 | convolution fusion | flops 755097280 | bytes 4818176 | tf_op jit(solution)/shard_map/dot_general | solution.py:86
  79.9 0.0 copy-done.1
  79.9 0.3 exponential_reduce_fusion
  80.2 25.1 %all-gather.5 = f32[8,3,320]{2,1,0:T(4,128)S(1)} all-gather(f32[1,3,320]{2,1,0:T(4,128)S(1)} %maximum_bitcast_fusion), channel_id=2, replica_groups=mesh['cls_0'=8,'cls_1'=2,'cls_2'=2,'dp_0'=8,'dp_1'=2] {'cls_0'}, dimensions={0}, use_global_device_ids=true | all-gather | bytes 34560 | tf_op jit(solution)/shard_map/all_gather | solution.py:37
  105.4 4.7 %all-gather.6 = f32[2,3,320]{2,1,0:T(4,128)S(1)} all-gather(f32[1,3,320]{2,1,0:T(4,128)S(1)} %maximum_bitcast_fusion.1), channel_id=3, replica_groups=mesh['cls_0'=8,'cls_1'=2,'cls_2'=2,'dp_0'=8,'dp_1'=2] {'cls_1'}, dimensions={0}, use_global_device_ids=true | all-gather | bytes 11520 | tf_op jit(solution)/shard_map/all_gather | solution.py:37
  110.2 11.2 %all-gather.7 = f32[2,3,320]{2,1,0:T(4,128)S(1)} all-gather(f32[1,3,320]{2,1,0:T(4,128)S(1)} %maximum_bitcast_fusion.2), channel_id=4, replica_groups=mesh['cls_0'=8,'cls_1'=2,'cls_2'=2,'dp_0'=8,'dp_1'=2] {'cls_2'}, dimensions={0}, use_global_device_ids=true | all-gather | bytes 11520 | tf_op jit(solution)/shard_map/all_gather | solution.py:37
  121.4 18.5 %all-gather.8 = f32[8,3,320]{2,1,0:T(4,128)S(1)} all-gather(f32[1,3,320]{2,1,0:T(4,128)S(1)} %maximum_bitcast_fusion.3), channel_id=5, replica_groups=mesh['cls_0'=8,'cls_1'=2,'cls_2'=2,'dp_0'=8,'dp_1'=2] {'dp_0'}, dimensions={0}, use_global_device_ids=true | all-gather | bytes 34560 | tf_op jit(solution)/shard_map/all_gather | solution.py:37
  140.0 3.2 %all-gather.9 = f32[2,3,320]{2,1,0:T(4,128)S(1)} all-gather(f32[1,3,320]{2,1,0:T(4,128)S(1)} %maximum_bitcast_fusion.4), channel_id=6, replica_groups=mesh['cls_0'=8,'cls_1'=2,'cls_2'=2,'dp_0'=8,'dp_1'=2] {'dp_1'}, dimensions={0}, use_global_device_ids=true | all-gather | bytes 11520 | tf_op jit(solution)/shard_map/all_gather | solution.py:37
  143.3 0.6 add_subtract_fusion
  143.9 3.2 %fusion.74 = f32[320,3072]{1,0:T(8,128)} fusion(bf16[384,3072]{1,0:T(8,128)(2,1)S(1)} %copy-done, f32[320,384]{1,0:T(8,128)S(1)} %get-tuple-element.22, f32[320]{0:T(512)S(1)} %get-tuple-element.11, f32[320]{0:T(512)S(1)} %get-tuple-element.12, f32[320]{0:T(512)S(1)} %copy-done.2, s32[384]{0:T(512)S(1)} %iota_add_fusion, s32[320]{0:T(512)S(1)} %copy-done.1), kind=kOutput, calls=%fused_computation.148 | convolution fusion | flops 755834880 | bytes 6789632 | tf_op jit(solution)/shard_map/dot_general | solution.py:107
  147.1 0.0 reduce-scatter.4.cloned.1.call-update
  147.1 57.5 %reduce-scatter.4.cloned.1.call-done = f32[40,3072]{1,0:T(8,128)} async-done(((f32[320,3072]{1,0:T(8,128)}), f32[40,3072]{1,0:T(8,128)}) %reduce-scatter.4.cloned.1.call-update) | async-done | bytes 491536 | tf_op jit(solution)/shard_map/reduce_scatter | solution.py:57
  204.6 11.2 %fusion = f32[24,3072]{1,0:T(8,128)S(1)} fusion(f32[40,3072]{1,0:T(8,128)} %reduce-scatter.4.cloned.1.call-done), kind=kCustom, calls=%all-reduce-scatter | all-reduce-scatter fusion | flops 147457 | bytes 788480
  215.8 2.8 %collective-permute-start = (f32[4,3072]{1,0:T(4,128)S(1)}, f32[4,3072]{1,0:T(4,128)}, u32[]{:S(2)}, u32[]{:S(2)}) collective-permute-start(f32[4,3072]{1,0:T(4,128)S(1)} %slice.477), channel_id=1, source_target_pairs={{0,1},{2,3},{4,5},{6,7},{8,9},{10,11},{12,13},{14,15},{16,17},{18,... | collective-permute-start | bytes 147464
  218.6 1.3 dynamic-slice.4
  220.5 0.0 collective-permute-done
  220.5 1.1 concatenate.20
  221.6 0.7 constant_dynamic-slice_fusion
  222.4 1.1 reshape.1287
  223.5 0.9 copy.9
  224.4 12.1 %all-to-all-start.1 = ((f32[32,20,96]{2,1,0:T(8,128)}), f32[32,20,96]{2,1,0:T(8,128)S(1)}, u32[]{:S(2)}, u32[]{:S(2)}) async-start(f32[32,20,96]{2,1,0:T(8,128)} %bitcast.392), calls=%async_computation.2 | async-start | bytes 786432 | tf_op jit(solution)/shard_map/all_to_all | solution.py:69
  236.5 1.3 dynamic_slice.3
  237.8 4.6 %convolution_convert_fusion = bf16[384,3072]{1,0:T(8,128)(2,1)} fusion(bf16[320,3072]{1,0:T(8,128)(2,1)} %reshape.1283, f32[320,384]{1,0:T(8,128)S(1)} %get-tuple-element.22, f32[320]{0:T(512)S(1)} %get-tuple-element.11, f32[320]{0:T(512)S(1)} %get-tuple-element.12, f32[320]{0:T(512)S(1)} %copy-done.2, s32[384]{0:T(512)} %copy-done.3, s32[320]{0:T(512)S(1)} %copy-done.1), kind=kOutput, calls=%fused_computation | convolution fusion | flops 757014528 | bytes 4823552 | tf_op jit(solution)/shard_map/dot_general | solution.py:103
  242.4 8.4 %all-to-all-done.1 = f32[32,20,96]{2,1,0:T(8,128)S(1)} async-done(((f32[32,20,96]{2,1,0:T(8,128)}), f32[32,20,96]{2,1,0:T(8,128)S(1)}, u32[]{:S(2)}, u32[]{:S(2)}) %all-to-all-start.1) | async-done | bytes 245792 | tf_op jit(solution)/shard_map/all_to_all | solution.py:69
  250.7 0.6 reduce_sum.29
  (24 shorter events, 0.3 us)
Async XLA Ops:
  7.2 69.8 %copy-start = (bf16[384,3072]{1,0:T(8,128)(2,1)S(1)}, bf16[384,3072]{1,0:T(8,128)(2,1)}, u32[]{:S(2)}) copy-start(bf16[384,3072]{1,0:T(8,128)(2,1)} %param.5) | copy-start | bytes 7077892
  9.9 63.1 %all-to-all-start = ((bf16[16,20,3072]{2,1,0:T(8,128)(2,1)}), bf16[16,20,3072]{2,1,0:T(8,128)(2,1)}, u32[]{:S(2)}, u32[]{:S(2)}) async-start(bf16[16,20,3072]{2,1,0:T(8,128)(2,1)} %broadcast_in_dim.4), calls=%async_computation | async-start | bytes 4718592 | tf_op jit(solution)/shard_map/all_to_all | solution.py:20
  18.6 185.9 %reduce-scatter.4.cloned.1.call-start = ((), (), s32[]{:S(2)}) async-start(), calls=%async_computation.3 | async-start | bytes 4423680 | tf_op jit(solution)/shard_map/reduce_scatter | solution.py:57
  18.7 125.2 %copy-start.3 = (s32[384]{0:T(512)}, s32[384]{0:T(512)S(1)}, u32[]{:S(2)}) copy-start(s32[384]{0:T(512)S(1)} %iota_add_fusion) | copy-start | bytes 4612
  77.0 2.9 %copy-start.1 = (s32[320]{0:T(512)S(1)}, s32[320]{0:T(512)}, u32[]{:S(2)}) copy-start(s32[320]{0:T(512)} %param.6) | copy-start | bytes 3844
  77.0 66.9 %copy-start.2 = (f32[320]{0:T(512)S(1)}, f32[320]{0:T(512)}, u32[]{:S(2)}) copy-start(f32[320]{0:T(512)} %param.7) | copy-start | bytes 3844
  215.8 4.7 %collective-permute-start = (f32[4,3072]{1,0:T(4,128)S(1)}, f32[4,3072]{1,0:T(4,128)}, u32[]{:S(2)}, u32[]{:S(2)}) collective-permute-start(f32[4,3072]{1,0:T(4,128)S(1)} %slice.477), channel_id=1, source_target_pairs={{0,1},{2,3},{4,5},{6,7},{8,9},{10,11},{12,13},{14,15},{16,17},{18,... | collective-permute-start | bytes 147464
  224.4 26.3 %all-to-all-start.1 = ((f32[32,20,96]{2,1,0:T(8,128)}), f32[32,20,96]{2,1,0:T(8,128)S(1)}, u32[]{:S(2)}, u32[]{:S(2)}) async-start(f32[32,20,96]{2,1,0:T(8,128)} %bitcast.392), calls=%async_computation.2 | async-start | bytes 786432 | tf_op jit(solution)/shard_map/all_to_all | solution.py:69
Sparse Core Ops, SparseCore 0:
  147.2 57.2 reduce-scatter.3
where the time goes:
time: 259 us; the launch traced here: 258 us
  waiting for transfers between devices  120 us (46%)
  blocking collectives  74 us (29%)
  starting transfers between devices  23.7 us (9%)
  between operations  14.9 us (6%)
  local copies, waits for them, and re-layouts  13.2 us (5%)
  matrix products  10.6 us (4%)
    all_gather x5, blocking collectives, collected_together(): both, at, found = (lax.all_gather(jnp.concatenate(lines), axis), 0, {})  62.8 us
    reduce_scatter x1, waiting for transfers between devices, summed_rows_2(): so_far = lax.psum_scatter(so_far, axis, scatter_dimension=0, tiled=True)  57.5 us
    all_to_all x1, waiting for transfers between devices, copy_for_each(): lax.all_to_all(jnp.broadcast_to(shard[None], (peers, *shard.shape)), axis...  54.3 us
    all_to_all x1, starting transfers between devices, summed_on_arrival(): lax.all_to_all(pieces, axis, split_axis=0, concat_axis=0, tiled=True)  12.1 us
    unnamed x1, blocking collectives  11.2 us
    all_to_all x1, starting transfers between devices, copy_for_each(): lax.all_to_all(jnp.broadcast_to(shard[None], (peers, *shard.shape)), axis...  8.72 us
    all_to_all x1, waiting for transfers between devices, summed_on_arrival(): lax.all_to_all(pieces, axis, split_axis=0, concat_axis=0, tiled=True)  8.36 us
  transfers between devices with their start and end apart: 4, of which 3 were waited for; matrix products, arithmetic and copies ran while one was open for 3% of the time, Pallas kernels for 0%

commit v1 on v0

v1 whole, which is shorter than its diff:
```python
import jax
import jax.numpy as jnp
from jax import lax
from jax.experimental import pallas as pl
from jax.experimental.pallas import tpu as pltpu
from jax.sharding import Mesh
from jax.sharding import PartitionSpec as P

CLS = ("cls_0", "cls_1", "cls_2")
DP = ("dp_0", "dp_1")
CLS_DP = ("cls_0", "cls_1", "cls_2", "dp_0", "dp_1")
MESH = pl.DeviceIdType.MESH
F32 = jnp.float32
BF16 = jnp.bfloat16

RING = 8
SHARDS = 16
D = 3072
ROWS = 384
TOK = 320
MAIN = 256
REST = 64
HALF = D // 2
PACK = HALF + HALF // 4
SUB = ((0, 1024), (1024, PACK - 1024))
BLK = 384
RIGHT = RING // 2
LEFT = RING - 1 - RIGHT
ORDER = (4, 5, 3, 6, 2, 7, 1, 0)


def nt(a, b):
    return lax.dot_general(a, b, (((1,), (1,)), ((), ())), preferred_element_type=F32)


def tn(a, b):
    return lax.dot_general(a, b, (((0,), (0,)), ((), ())), preferred_element_type=F32)


def nn(a, b):
    return lax.dot_general(a, b, (((1,), (0,)), ((), ())), preferred_element_type=F32)


def kernel(
    hid, w_hbm, labels, cot, loss_out, wg_out, hg_out,
    w, g, xr, lt, gt, stat_send, stat_recv, pb, rb, send_r, send_l, recv_r, recv_l,
    f32buf, f_send, f_recv, s_send, s_recv, wg,
    w_sem, wg_sem, ring_s, ring_v, x_s, x_v, d_s, d_v, st_s, st_v, c_s, c_v, rr_s, rr_v, f_s, f_v, e_s, e_v,
):
    z, xh, c = lax.axis_index("cls_0"), lax.axis_index("cls_1"), lax.axis_index("cls_2")
    y, xl = lax.axis_index("dp_0"), lax.axis_index("dp_1")
    x = xh * 2 + xl
    me = y * 2 + xl

    def at_y(d):
        return {"dp_0": (y + d) % RING}

    def at_z(d):
        return {"cls_0": (z + d) % RING}

    def at_x(dx, dc):
        there = (x + dx) % 4
        return {"cls_1": there // 2, "dp_1": there % 2, "cls_2": (c + dc) % 2}

    partner = {"cls_2": 1 - c}

    def copy(src, dst, s, v, device):
        return pltpu.make_async_remote_copy(
            src_ref=src, dst_ref=dst, send_sem=s, recv_sem=v, device_id=device, device_id_type=MESH
        )

    load_w = pltpu.make_async_copy(w_hbm, w, w_sem)
    load_w.start()

    barrier = pltpu.get_barrier_semaphore()
    others = [(dx, dc) for dx in range(4) for dc in range(2) if dx or dc]
    peers = [at_x(dx, dc) for dx, dc in others]
    peers += [at_y(d) for d in range(1, RING)] + [at_z(d) for d in range(1, RING)]
    for peer in peers:
        pl.semaphore_signal(barrier, inc=1, device_id=peer, device_id_type=MESH)
    pl.semaphore_wait(barrier, len(peers))

    sent = []

    def shard(o, own):
        return ((y + o) % RING) * 2 + (xl if own else 1 - xl)

    def part(o, own, h, sub):
        return g.at[shard(o, own), h, :, pl.ds(*SUB[sub])]

    def begin(d):
        d.start()
        sent.append(d)

    def source(o, sub):
        return hid.at[c, :, pl.ds(*SUB[sub])] if o == 0 else part(o, True, c, sub)

    def ring(side, step, sub):
        o = -step if side == 0 else step
        begin(copy(source(o, sub), part(o, True, c, sub), ring_s.at[side, step, sub],
                   ring_v.at[side, step, sub], at_y(1 if side == 0 else -1)))

    def spread_x(o, sub):
        begin(copy(source(o, sub), part(o, True, c, sub), x_s.at[o % RING, sub],
                   x_v.at[o % RING, sub], at_x(1 if sub == 0 else 3, 0)))

    def spread_core(o, own, sub):
        begin(copy(part(o, own, c, sub), part(o, own, c, sub), d_s.at[o % RING, int(own), sub],
                   d_v.at[o % RING, int(own), sub], partner))

    def arrived(ref, s, v):
        copy(ref, ref, s, v, partner).wait_recv()

    for sub in range(2):
        ring(0, 0, sub)
        ring(1, 0, sub)
        spread_x(0, sub)
    g[me] = hid[...]

    def from_x(o):
        for sub in range(2):
            arrived(part(o, False, c, sub), x_s.at[o % RING, sub], x_v.at[o % RING, sub])
            spread_core(o, False, sub)

    waiting = [0]
    for step in range(RIGHT):
        got = []
        for sub in range(2):
            for side in range(2):
                if side == 1 and step >= LEFT:
                    continue
                o = -(step + 1) if side == 0 else step + 1
                arrived(part(o, True, c, sub), ring_s.at[side, step, sub], ring_v.at[side, step, sub])
                if step + 1 < (RIGHT if side == 0 else LEFT):
                    ring(side, step + 1, sub)
                spread_x(o, sub)
                spread_core(o, True, sub)
                if sub == 1:
                    got.append(o)
        for o in waiting:
            from_x(o)
        waiting = got
    for o in waiting:
        from_x(o)
    for o in [0] + [k for step in range(RIGHT) for k in (-(step + 1), step + 1)][: RING - 1]:
        for own in (True, False):
            if o == 0 and own:
                continue
            for sub in range(2):
                arrived(part(o, own, 1 - c, sub), d_s.at[o % RING, int(own), sub], d_v.at[o % RING, int(own), sub])
    load_w.wait()

    to = lax.broadcasted_iota(jnp.int32, (MAIN, MAIN), 0)
    source_row = lax.broadcasted_iota(jnp.int32, (MAIN, MAIN), 1)
    perm = (source_row == ((to & 63) >> 2) * 16 + (to >> 6) * 4 + (to & 3)).astype(F32).astype(BF16)
    col = lax.broadcasted_iota(jnp.int32, (BLK, 512), 0)
    lane = lax.broadcasted_iota(jnp.int32, (BLK, 512), 1)
    fold = ((col == (lane >> 7) * 96 + (lane & 127)) & ((lane & 127) < 96)).astype(F32).astype(BF16)

    for h in range(2):
        rest = nn(perm, g[:, h, :, HALF:PACK].reshape(MAIN, HALF // 4)).astype(BF16)
        for b in range(4):
            xr[:, h * HALF + b * 384 : h * HALF + (b + 1) * 384] = rest[b * REST : (b + 1) * REST]

    def main_rows(h):
        return g[:, h, :, :HALF].reshape(MAIN, HALF)

    lt[:, :MAIN] = nt(w[:, :HALF], main_rows(0)) + nt(w[:, HALF:], main_rows(1))
    lt[:, MAIN:] = nt(w[...], xr[...])

    offset = ((z * 4 + xh * 2 + c) * SHARDS + me) * ROWS
    classes = offset + lax.broadcasted_iota(jnp.int32, (ROWS, TOK), 0)
    chosen = classes == labels[...]
    logits = lt[...]
    peak = jnp.max(logits, axis=0, keepdims=True)
    total = jnp.sum(jnp.exp(logits - peak), axis=0, keepdims=True)
    picked = jnp.sum(jnp.where(chosen, logits, 0.0), axis=0, keepdims=True)

    first = 0
    for devices in (peers[:7], peers[7:14], peers[14:]):
        phase = first // 7
        stat_send[phase, :, 0:TOK] = peak
        stat_send[phase, :, 384 : 384 + TOK] = total
        stat_send[phase, :, 768 : 768 + TOK] = picked
        for j, device in enumerate(devices):
            begin(copy(stat_send.at[phase], stat_recv.at[first + j], st_s.at[first + j], st_v.at[first + j], device))
        parts = [(peak, total, picked)]
        for j in range(7):
            arrived(stat_recv.at[first + j], st_s.at[first + j], st_v.at[first + j])
            parts.append((
                stat_recv[first + j, :, 0:TOK],
                stat_recv[first + j, :, 384 : 384 + TOK],
                stat_recv[first + j, :, 768 : 768 + TOK],
            ))
        peak = parts[0][0]
        for p in parts[1:]:
            peak = jnp.maximum(peak, p[0])
        total = sum(p[1] * jnp.exp(p[0] - peak) for p in parts)
        picked = sum(p[2] for p in parts)
        first += 7

    loss_out[...] = peak + jnp.log(total) - picked
    soft = jnp.exp(lt[...] - peak) / total
    gt[...] = (cot[...] * (soft - chosen.astype(F32))).astype(BF16)

    for k in range(RING):
        columns = slice(k * BLK, (k + 1) * BLK)
        main = tn(gt[:, :MAIN], w[:, columns]).astype(BF16).reshape(RING, 2, 16, BLK)
        pb[0, :, k] = main[..., :256]
        pb[1, k, :, :, :, 0:128] = main[..., 256:]
        rest = tn(gt[:, MAIN:], w[:, columns]).astype(BF16)
        folded = nn(rest, fold).astype(BF16)
        stacked = jnp.concatenate([folded[:, b * 128 : (b + 1) * 128] for b in range(4)], axis=0)
        pb[1, k, :, :, :, 128:256] = tn(perm, stacked).astype(BF16).reshape(RING, 2, 16, 128)

    pos = (1 - c) * y + c * z
    pos2 = (1 - c) * z + c * y

    def along(d):
        return {"dp_0": (y + (1 - c) * d) % RING, "cls_0": (z + c * d) % RING}

    def across(d):
        return {"dp_0": (y + c * d) % RING, "cls_0": (z + (1 - c) * d) % RING}

    for j in ORDER:
        begin(copy(pb.at[1 - c, (pos2 + j) % RING], rb.at[j], c_s.at[j], c_v.at[j], partner))

    def weight_part(h, lo, hi):
        at = slice(h * HALF + lo, h * HALF + hi)
        wg[:, at] = (
            nn(gt[:, :MAIN], g[:, h, :, lo:hi].reshape(MAIN, hi - lo)) + nn(gt[:, MAIN:], xr[:, at])
        ).astype(BF16)

    pieces = [(h, lo, lo + 384) for h in range(2) for lo in range(0, HALF, 384)]

    def mine(j, sub):
        s = slice(sub * 4, sub * 4 + 4)
        return pb[c, (pos + j) % RING, s].astype(F32) + rb[j, s].astype(F32)

    def hop(side, step, sub):
        s = pl.ds(sub * 4, 4)
        out, into = (send_r, recv_r) if side == 0 else (send_l, recv_l)
        return copy(out.at[step, s], into.at[step, s], rr_s.at[side, step, sub], rr_v.at[side, step, sub],
                    along(1 if side == 0 else -1))

    def landed(ref, step, side, sub):
        arrived(ref.at[step, pl.ds(sub * 4, 4)], rr_s.at[side, step, sub], rr_v.at[side, step, sub])

    for step in range(RIGHT):
        for side in range(2):
            steps = RIGHT if side == 0 else LEFT
            if step >= steps:
                continue
            j = steps - step if side == 0 else RING - (steps - step)
            arrived(rb.at[j], c_s.at[j], c_v.at[j])
            for sub in range(2):
                s = slice(sub * 4, sub * 4 + 4)
                value = mine(j, sub)
                if step:
                    ref = recv_r if side == 0 else recv_l
                    landed(ref, step - 1, side, sub)
                    value = value + ref[step - 1, s].astype(F32)
                (send_r if side == 0 else send_l)[step, s] = value.astype(BF16)
                begin(hop(side, step, sub))
        for piece in pieces[2 * step : 2 * step + 2]:
            weight_part(*piece)
    store_wg = pltpu.make_async_copy(wg, wg_out, wg_sem)
    store_wg.start()

    arrived(rb.at[0], c_s.at[0], c_v.at[0])
    for sub in range(2):
        s = slice(sub * 4, sub * 4 + 4)
        landed(recv_l, LEFT - 1, 1, sub)
        landed(recv_r, RIGHT - 1, 0, sub)
        value = mine(0, sub) + recv_l[LEFT - 1, s].astype(F32) + recv_r[RIGHT - 1, s].astype(F32)
        f32buf[s] = value
        f_send[s] = value.astype(BF16)
    for d in (4, 3, 5, 2, 6, 1, 7):
        begin(copy(f_send.at[(pos2 + d) % RING], f_recv.at[d - 1], f_s.at[d - 1], f_v.at[d - 1], across(d)))
    value = f32buf[pos2]
    for d in (1, 7, 2, 6, 3, 5, 4):
        arrived(f_recv.at[d - 1], f_s.at[d - 1], f_v.at[d - 1])
        value = value + f_recv[d - 1].astype(F32)

    s_send[...] = value
    for j, (dx, dc) in enumerate(others):
        begin(copy(s_send.at[(x + dx) % 2], s_recv.at[j], e_s.at[j], e_v.at[j], at_x(dx, dc)))
    same, other = s_send[xl], None
    for j, (dx, dc) in enumerate(others):
        arrived(s_recv.at[j], e_s.at[j], e_v.at[j])
        if dc == 0:
            same = same + s_recv[j]
        else:
            other = s_recv[j] if other is None else other + s_recv[j]
    hg_out[c] = same
    hg_out[1 - c] = other

    for d in sent:
        d.wait_send()
    store_wg.wait()


def body(hidden, weight, labels, cotangent):
    wide = hidden[:16].reshape(16, 2, HALF).transpose(1, 0, 2)
    rest = hidden[16:].reshape(4, 2, 4, HALF // 4).transpose(1, 2, 0, 3).reshape(2, 16, HALF // 4)
    packed = jnp.concatenate([wide, rest], axis=2)

    def reorder(v):
        v = v.reshape(SHARDS, 20)
        return jnp.concatenate([v[:, :16].reshape(1, MAIN), v[:, 16:].reshape(1, REST)], axis=1)

    vmem = pl.BlockSpec(memory_space=pltpu.VMEM)
    hbm = pl.BlockSpec(memory_space=pl.ANY)
    dma = pltpu.SemaphoreType.DMA
    loss, weight_grad, hg = pl.pallas_call(
        kernel,
        out_shape=(
            jax.ShapeDtypeStruct((1, TOK), F32),
            jax.ShapeDtypeStruct((ROWS, D), BF16),
            jax.ShapeDtypeStruct((2, 16, 256), F32),
        ),
        in_specs=[vmem, hbm, vmem, vmem],
        out_specs=(vmem, hbm, vmem),
        scratch_shapes=[
            pltpu.VMEM((ROWS, D), BF16),
            pltpu.VMEM((SHARDS, 2, 16, PACK), BF16),
            pltpu.VMEM((REST, D), BF16),
            pltpu.VMEM((ROWS, TOK), F32),
            pltpu.VMEM((ROWS, TOK), BF16),
            pltpu.VMEM((3, 1, 1152), F32),
            pltpu.VMEM((21, 1, 1152), F32),
            pltpu.VMEM((2, RING, RING, 2, 16, 256), BF16),
            pltpu.VMEM((RING, RING, 2, 16, 256), BF16),
            pltpu.VMEM((RIGHT, RING, 2, 16, 256), BF16),
            pltpu.VMEM((LEFT, RING, 2, 16, 256), BF16),
            pltpu.VMEM((RIGHT, RING, 2, 16, 256), BF16),
            pltpu.VMEM((LEFT, RING, 2, 16, 256), BF16),
            pltpu.VMEM((RING, 2, 16, 256), F32),
            pltpu.VMEM((RING, 2, 16, 256), BF16),
            pltpu.VMEM((RING - 1, 2, 16, 256), BF16),
            pltpu.VMEM((2, 16, 256), F32),
            pltpu.VMEM((7, 16, 256), F32),
            pltpu.VMEM((ROWS, D), BF16),
            dma, dma,
            dma((2, RIGHT, 2)), dma((2, RIGHT, 2)),
            dma((RING, 2)), dma((RING, 2)),
            dma((RING, 2, 2)), dma((RING, 2, 2)),
            dma((21,)), dma((21,)),
            dma((RING,)), dma((RING,)),
            dma((2, RIGHT, 2)), dma((2, RIGHT, 2)),
            dma((RING - 1,)), dma((RING - 1,)),
            dma((7,)), dma((7,)),
        ],
        compiler_params=pltpu.CompilerParams(
            collective_id=0, has_side_effects=True, vmem_limit_bytes=48 * 1024 * 1024
        ),
        name="step",
    )(packed, weight, reorder(labels), reorder(cotangent))

    me = lax.axis_index(DP)
    token_loss = jnp.concatenate([
        lax.dynamic_slice(loss[0], (me * 16,), (16,)),
        lax.dynamic_slice(loss[0], (MAIN + me * 4,), (4,)),
    ])
    block = lax.axis_index("cls_1") * 2 + lax.axis_index("cls_2")
    main = jnp.concatenate([hg[0], hg[1, :, :128]], axis=1)
    main = lax.dynamic_slice(main, (0, block * 96), (16, 96))
    rest = lax.dynamic_slice(hg[1], (block * 4, 128), (4, 96))
    hidden_grad = jnp.concatenate([main, rest], axis=0).astype(BF16)
    return (token_loss, weight_grad, hidden_grad)


def solution(mesh):
    torus = Mesh(mesh.devices.reshape(8, 2, 2, 8, 2), ("cls_0", "cls_1", "cls_2", "dp_0", "dp_1"))
    in_specs = (P(DP, None), P(CLS_DP, None), P(), P())
    out_specs = (P(DP), P(CLS_DP, None), P(DP, CLS))
    return jax.shard_map(body, mesh=torus, in_specs=in_specs, out_specs=out_specs, check_vma=False)
```

time: 259 us -> 86.9 us (0.34)
  waiting for transfers between devices: 120 us -> 0 us
  Pallas kernels: 0 us -> 77.6 us
  blocking collectives: 74 us -> 0 us
  starting transfers between devices: 23.7 us -> 0 us
  between operations: 14.9 us -> 0.72 us
  matrix products: 10.6 us -> 0 us
  local copies, waits for them, and re-layouts: 13.2 us -> 6.98 us
    pallas_call x0 -> x1, Pallas kernels: none -> 77.6 us  [body(): pl.pallas_call(kernel, out_shape=(jax.ShapeDtypeStruct((1, TOK), F32), ja...]
    all_gather x5 -> x0, blocking collectives: 62.8 us -> none  [collected_together(): both, at, found = (lax.all_gather(jnp.concatenate(lines), axis), 0, {})]
    all_to_all x2 -> x0, waiting for transfers between devices: 62.7 us -> none  [the longest x1 54.3 us: copy_for_each(): lax.all_to_all(jnp.broadcast_to(shard[None], (peers, *shard.shape)), axis...]
    reduce_scatter x1 -> x0, waiting for transfers between devices: 57.5 us -> none  [summed_rows_2(): so_far = lax.psum_scatter(so_far, axis, scatter_dimension=0, tiled=True)]
    all_to_all x2 -> x0, starting transfers between devices: 20.8 us -> none  [the longest x1 12.1 us: summed_on_arrival(): lax.all_to_all(pieces, axis, split_axis=0, concat_axis=0, tiled=True)]
    unnamed x1 -> x0, blocking collectives: 11.2 us -> none
    dot_general x3 -> x0, matrix products: 10.6 us -> none  [the longest x1 4.57 us: body(): lax.dot_general(grad_logits, gathered, (((0,), (0,)), ((), ())), preferre...]
    reshape x6 -> x8, local copies, waits for them, and re-layouts: 6 us -> 1.89 us  [the longest x2 1.53 us: reorder(): v = v.reshape(SHARDS, 20)]
  transfers between devices with their start and end apart: 4 -> 0, of which waited for: 3 -> 0; matrix products, arithmetic and copies ran while one was open for 3% -> 0% of each run, Pallas kernels for 0% -> 0%
where the time goes in v1:
time: 86.9 us; the launch traced here: 86.6 us
  Pallas kernels  77.6 us (89%)
  local copies, waits for them, and re-layouts  6.98 us (8%)
  other arithmetic  1.32 us (2%)
    pallas_call x1, Pallas kernels, body(): pl.pallas_call(kernel, out_shape=(jax.ShapeDtypeStruct((1, TOK), F32), ja...  77.6 us
    unnamed x3, local copies, waits for them, and re-layouts  3.07 us

profile of v1, /device:TPU:1, one launch (start us, length us, event | category | flops | bytes accessed | tf_op | source)
XLA Modules:
  0.0 86.6 jit_solution(1035620734813373558)
XLA Ops:
  0.6 0.8 reshape.40
  1.4 0.1 slice.37
  1.5 0.1 reshape.42
  1.6 0.1 reshape.41
  1.7 0.8 reshape.43
  2.4 0.1 slice.39
  2.5 0.1 reshape.45
  2.6 0.1 reshape.44
  2.7 0.9 %slice.27 = bf16[16,3072]{1,0:T(8,128)(2,1)S(1)} slice(bf16[20,3072]{1,0:T(8,128)(2,1)} %param.4), slice={[0:16], [0:3072]} | slice | bytes 196608 | tf_op jit(solution)/shard_map/slice | solution.py:304
  3.6 0.8 slice.28
  4.5 0.0 copy-start
  4.5 1.7 %copy-done = bf16[384,3072]{1,0:T(8,128)(2,1)S(1)} copy-done((bf16[384,3072]{1,0:T(8,128)(2,1)S(1)}, bf16[384,3072]{1,0:T(8,128)(2,1)}, u32[]{:S(2)}) %copy-start) | copy-done | bytes 2359320
  6.1 77.6 %step.1 = (f32[1,320]{1,0:T(1,128)S(1)}, bf16[384,3072]{1,0:T(8,128)(2,1)S(1)}, f32[2,16,256]{2,1,0:T(8,128)S(1)}) custom-call(bf16[2,16,1920]{2,1,0:T(8,128)(2,1)S(1)} %pad_maximum_fusion.hid, bf16[384,3072]{1,0:T(8,128)(2,1)S(1)} %copy-done, s32[1,320]{1,0:T(1,128)S(1)} %pad_add_fusion.labels, f32[1,320]{1,0:T(1,128)S(1)} %pad_maximum_fusion.2.cot), custom_call_target="tpu_custom_call" | custom-call | tf_op jit(solution)/shard_map/step/pallas_call | solution.py:315
  83.7 0.1 fusion.1
  83.8 0.6 pad_maximum_fusion.1
  84.4 0.1 fusion.3
  84.5 0.1 fusion.4
  84.6 0.6 pad_maximum_fusion.3
  85.2 1.4 %copy.14 = bf16[384,3072]{1,0:T(8,128)(2,1)} copy(bf16[384,3072]{1,0:T(8,128)(2,1)S(1)} %get-tuple-element.15) | data formatting | bytes 4718592
  (8 shorter events, 0.1 us)
Async XLA Ops:
  4.5 1.7 %copy-start = (bf16[384,3072]{1,0:T(8,128)(2,1)S(1)}, bf16[384,3072]{1,0:T(8,128)(2,1)}, u32[]{:S(2)}) copy-start(bf16[384,3072]{1,0:T(8,128)(2,1)} %w_hbm.1) | copy-start | bytes 7077892

commit v2 on v1

v2 whole, which is shorter than its diff:
```python
import jax
import jax.numpy as jnp
from jax import lax
from jax.experimental import pallas as pl
from jax.experimental.pallas import tpu as pltpu
from jax.sharding import Mesh
from jax.sharding import PartitionSpec as P

CLS = ("cls_0", "cls_1", "cls_2")
DP = ("dp_0", "dp_1")
CLS_DP = ("cls_0", "cls_1", "cls_2", "dp_0", "dp_1")
MESH = pl.DeviceIdType.MESH
F32 = jnp.float32
BF16 = jnp.bfloat16

RING = 8
SHARDS = 16
D = 3072
ROWS = 384
TOK = 320
MAIN = 256
REST = 64
HALF = D // 2
PACK = HALF + HALF // 4
SUB = ((0, 1024), (1024, PACK - 1024))
BLK = 384
RIGHT = RING // 2
LEFT = RING - 1 - RIGHT
ORDER = (4, 5, 3, 6, 2, 7, 1, 0)


def nt(a, b):
    return lax.dot_general(a, b, (((1,), (1,)), ((), ())), preferred_element_type=F32)


def tn(a, b):
    return lax.dot_general(a, b, (((0,), (0,)), ((), ())), preferred_element_type=F32)


def nn(a, b):
    return lax.dot_general(a, b, (((1,), (0,)), ((), ())), preferred_element_type=F32)


def kernel(
    hid, w_hbm, labels, cot, loss_out, wg, hg_out,
    w, g, xr, lt, gt, per_token, stat_send, stat_recv, pb, rb, send_r, send_l, recv_r, recv_l,
    f32buf, f_send, f_recv, s_send, s_recv,
    w_sem, ring_s, ring_v, x_s, x_v, d_s, d_v, st_s, st_v, c_s, c_v, rr_s, rr_v, f_s, f_v, e_s, e_v,
):
    z, xh, c = lax.axis_index("cls_0"), lax.axis_index("cls_1"), lax.axis_index("cls_2")
    y, xl = lax.axis_index("dp_0"), lax.axis_index("dp_1")
    x = xh * 2 + xl
    me = y * 2 + xl

    def at_y(d):
        return {"dp_0": (y + d) % RING}

    def at_z(d):
        return {"cls_0": (z + d) % RING}

    def at_x(dx, dc):
        there = (x + dx) % 4
        return {"cls_1": there // 2, "dp_1": there % 2, "cls_2": (c + dc) % 2}

    partner = {"cls_2": 1 - c}

    def copy(src, dst, s, v, device):
        return pltpu.make_async_remote_copy(
            src_ref=src, dst_ref=dst, send_sem=s, recv_sem=v, device_id=device, device_id_type=MESH
        )

    load_w = pltpu.make_async_copy(w_hbm, w, w_sem)
    load_w.start()

    with jax.named_scope("barrier"):
        barrier = pltpu.get_barrier_semaphore()
        others = [(dx, dc) for dx in range(4) for dc in range(2) if dx or dc]
        peers = [at_x(dx, dc) for dx, dc in others]
        peers += [at_y(d) for d in range(1, RING)] + [at_z(d) for d in range(1, RING)]
        for peer in peers:
            pl.semaphore_signal(barrier, inc=1, device_id=peer, device_id_type=MESH)

        tail = hid[16:20].astype(F32)
        for h in range(2):
            g[me, h, :, :HALF] = hid[0:16, h * HALF : (h + 1) * HALF]
            base = h * HALF
            quarters = [tail[:, base + b * 384 : base + (b + 1) * 384] for b in range(4)]
            g[me, h, :, HALF:] = jnp.concatenate(quarters, axis=0).astype(BF16)
        pl.semaphore_wait(barrier, len(peers))

    sent = []

    def shard(o, own):
        return ((y + o) % RING) * 2 + (xl if own else 1 - xl)

    def part(o, own, h, sub):
        return g.at[shard(o, own), h, :, pl.ds(*SUB[sub])]

    def begin(d):
        d.start()
        sent.append(d)

    def ring(side, step, sub):
        o = -step if side == 0 else step
        begin(copy(part(o, True, c, sub), part(o, True, c, sub), ring_s.at[side, step, sub],
                   ring_v.at[side, step, sub], at_y(1 if side == 0 else -1)))

    def spread_x(o, sub):
        begin(copy(part(o, True, c, sub), part(o, True, c, sub), x_s.at[o % RING, sub],
                   x_v.at[o % RING, sub], at_x(1 if sub == 0 else 3, 0)))

    def spread_core(o, own, sub):
        begin(copy(part(o, own, c, sub), part(o, own, c, sub), d_s.at[o % RING, int(own), sub],
                   d_v.at[o % RING, int(own), sub], partner))

    def arrived(ref, s, v):
        copy(ref, ref, s, v, partner).wait_recv()

    with jax.named_scope("own"):
        for sub in range(2):
            ring(0, 0, sub)
            ring(1, 0, sub)
            spread_x(0, sub)

        lab, ct = labels[...], cot[...]
        ct_1 = ct.astype(BF16).astype(F32)
        ct_2 = (ct - ct_1).astype(BF16).astype(F32)
        rows = [(lab & 255).astype(F32), ((lab >> 8) & 255).astype(F32), (lab >> 16).astype(F32), ct_1, ct_2, ct - ct_1 - ct_2]
        per_token[...] = jnp.zeros_like(per_token)
        for k, row in enumerate(rows):
            per_token[k : k + 1] = row
        natural = lax.broadcasted_iota(jnp.int32, (TOK, TOK), 0)
        spot = lax.broadcasted_iota(jnp.int32, (TOK, TOK), 1)
        other = spot - MAIN
        holds = jnp.where(spot < MAIN, (spot >> 4) * 20 + (spot & 15), (other >> 2) * 20 + 16 + (other & 3))
        per_token[...] = nn(per_token[...].astype(BF16), (natural == holds).astype(F32).astype(BF16))

    def from_x(o):
        for sub in range(2):
            arrived(part(o, False, c, sub), x_s.at[o % RING, sub], x_v.at[o % RING, sub])
            spread_core(o, False, sub)

    with jax.named_scope("ring_gather"):
        waiting = [0]
        for step in range(RIGHT):
            got = []
            for sub in range(2):
                for side in range(2):
                    if side == 1 and step >= LEFT:
                        continue
                    o = -(step + 1) if side == 0 else step + 1
                    arrived(part(o, True, c, sub), ring_s.at[side, step, sub], ring_v.at[side, step, sub])
                    if step + 1 < (RIGHT if side == 0 else LEFT):
                        ring(side, step + 1, sub)
                    spread_x(o, sub)
                    spread_core(o, True, sub)
                    if sub == 1:
                        got.append(o)
            for o in waiting:
                from_x(o)
            waiting = got
        for o in waiting:
            from_x(o)
    with jax.named_scope("core_gather"):
        for o in [0] + [k for step in range(RIGHT) for k in (-(step + 1), step + 1)][: RING - 1]:
            for own in (True, False):
                if o == 0 and own:
                    continue
                for sub in range(2):
                    arrived(part(o, own, 1 - c, sub), d_s.at[o % RING, int(own), sub], d_v.at[o % RING, int(own), sub])
        load_w.wait()

    to = lax.broadcasted_iota(jnp.int32, (MAIN, MAIN), 0)
    source_row = lax.broadcasted_iota(jnp.int32, (MAIN, MAIN), 1)
    perm = (source_row == ((to & 63) >> 2) * 16 + (to >> 6) * 4 + (to & 3)).astype(F32).astype(BF16)
    col = lax.broadcasted_iota(jnp.int32, (BLK, 512), 0)
    lane = lax.broadcasted_iota(jnp.int32, (BLK, 512), 1)
    fold = ((col == (lane >> 7) * 96 + (lane & 127)) & ((lane & 127) < 96)).astype(F32).astype(BF16)

    with jax.named_scope("rest_rows"):
        for h in range(2):
            rest = nn(perm, g[:, h, :, HALF:PACK].reshape(MAIN, HALF // 4)).astype(BF16)
            for b in range(4):
                xr[:, h * HALF + b * 384 : h * HALF + (b + 1) * 384] = rest[b * REST : (b + 1) * REST]

    def main_rows(h):
        return g[:, h, :, :HALF].reshape(MAIN, HALF)

    with jax.named_scope("logits"):
        lt[:, :MAIN] = nt(w[:, :HALF], main_rows(0)) + nt(w[:, HALF:], main_rows(1))
        lt[:, MAIN:] = nt(w[...], xr[...])

    with jax.named_scope("local_stats"):
        offset = ((z * 4 + xh * 2 + c) * SHARDS + me) * ROWS
        classes = offset + lax.broadcasted_iota(jnp.int32, (ROWS, TOK), 0)
        label = per_token[0:1] + per_token[1:2] * 256.0 + per_token[2:3] * 65536.0
        chosen = classes == label.astype(jnp.int32)
        weight_of = per_token[3:4] + per_token[4:5] + per_token[5:6]
        logits = lt[...]
        peak = jnp.max(logits, axis=0, keepdims=True)
        total = jnp.sum(jnp.exp(logits - peak), axis=0, keepdims=True)
        picked = jnp.sum(jnp.where(chosen, logits, 0.0), axis=0, keepdims=True)

    with jax.named_scope("exchange"):
        first = 0
        for devices in (peers[:7], peers[7:14], peers[14:]):
            phase = first // 7
            stat_send[phase, :, 0:TOK] = peak
            stat_send[phase, :, 384 : 384 + TOK] = total
            stat_send[phase, :, 768 : 768 + TOK] = picked
            for j, device in enumerate(devices):
                begin(copy(stat_send.at[phase], stat_recv.at[first + j], st_s.at[first + j], st_v.at[first + j], device))
            parts = [(peak, total, picked)]
            for j in range(7):
                arrived(stat_recv.at[first + j], st_s.at[first + j], st_v.at[first + j])
                parts.append((
                    stat_recv[first + j, :, 0:TOK],
                    stat_recv[first + j, :, 384 : 384 + TOK],
                    stat_recv[first + j, :, 768 : 768 + TOK],
                ))
            peak = parts[0][0]
            for p in parts[1:]:
                peak = jnp.maximum(peak, p[0])
            total = sum(p[1] * jnp.exp(p[0] - peak) for p in parts)
            picked = sum(p[2] for p in parts)
            first += 7

    with jax.named_scope("grad"):
        loss_out[...] = peak + jnp.log(total) - picked
        soft = jnp.exp(lt[...] - peak) / total
        gt[...] = (weight_of * (soft - chosen.astype(F32))).astype(BF16)

    with jax.named_scope("partial"):
        for k in range(RING):
            columns = slice(k * BLK, (k + 1) * BLK)
            main = tn(gt[:, :MAIN], w[:, columns]).astype(BF16).reshape(RING, 2, 16, BLK)
            pb[0, :, k] = main[..., :256]
            pb[1, k, :, :, :, 0:128] = main[..., 256:]
            rest = tn(gt[:, MAIN:], w[:, columns]).astype(BF16)
            folded = nn(rest, fold).astype(BF16)
            stacked = jnp.concatenate([folded[:, b * 128 : (b + 1) * 128] for b in range(4)], axis=0)
            pb[1, k, :, :, :, 128:256] = tn(perm, stacked).astype(BF16).reshape(RING, 2, 16, 128)

    pos = (1 - c) * y + c * z
    pos2 = (1 - c) * z + c * y

    def along(d):
        return {"dp_0": (y + (1 - c) * d) % RING, "cls_0": (z + c * d) % RING}

    def across(d):
        return {"dp_0": (y + c * d) % RING, "cls_0": (z + (1 - c) * d) % RING}

    for j in ORDER:
        begin(copy(pb.at[1 - c, (pos2 + j) % RING], rb.at[j], c_s.at[j], c_v.at[j], partner))

    def weight_part(h, lo, hi):
        at = slice(h * HALF + lo, h * HALF + hi)
        wg[:, at] = (
            nn(gt[:, :MAIN], g[:, h, :, lo:hi].reshape(MAIN, hi - lo)) + nn(gt[:, MAIN:], xr[:, at])
        ).astype(BF16)

    pieces = [(h, lo, lo + 384) for h in range(2) for lo in range(0, HALF, 384)]

    def mine(j, sub):
        s = slice(sub * 4, sub * 4 + 4)
        return pb[c, (pos + j) % RING, s].astype(F32) + rb[j, s].astype(F32)

    def hop(side, step, sub):
        s = pl.ds(sub * 4, 4)
        out, into = (send_r, recv_r) if side == 0 else (send_l, recv_l)
        return copy(out.at[step, s], into.at[step, s], rr_s.at[side, step, sub], rr_v.at[side, step, sub],
                    along(1 if side == 0 else -1))

    def landed(ref, step, side, sub):
        arrived(ref.at[step, pl.ds(sub * 4, 4)], rr_s.at[side, step, sub], rr_v.at[side, step, sub])

    with jax.named_scope("ring_reduce"):
        for step in range(RIGHT):
            for side in range(2):
                steps = RIGHT if side == 0 else LEFT
                if step >= steps:
                    continue
                j = steps - step if side == 0 else RING - (steps - step)
                arrived(rb.at[j], c_s.at[j], c_v.at[j])
                for sub in range(2):
                    s = slice(sub * 4, sub * 4 + 4)
                    value = mine(j, sub)
                    if step:
                        ref = recv_r if side == 0 else recv_l
                        landed(ref, step - 1, side, sub)
                        value = value + ref[step - 1, s].astype(F32)
                    (send_r if side == 0 else send_l)[step, s] = value.astype(BF16)
                    begin(hop(side, step, sub))
            for piece in pieces[2 * step : 2 * step + 2]:
                weight_part(*piece)

    with jax.named_scope("ring_end"):
        arrived(rb.at[0], c_s.at[0], c_v.at[0])
        for sub in range(2):
            s = slice(sub * 4, sub * 4 + 4)
            landed(recv_l, LEFT - 1, 1, sub)
            landed(recv_r, RIGHT - 1, 0, sub)
            value = mine(0, sub) + recv_l[LEFT - 1, s].astype(F32) + recv_r[RIGHT - 1, s].astype(F32)
            f32buf[s] = value
            f_send[s] = value.astype(BF16)
    with jax.named_scope("across"):
        for d in (4, 3, 5, 2, 6, 1, 7):
            begin(copy(f_send.at[(pos2 + d) % RING], f_recv.at[d - 1], f_s.at[d - 1], f_v.at[d - 1], across(d)))
        value = f32buf[pos2]
        for d in (1, 7, 2, 6, 3, 5, 4):
            arrived(f_recv.at[d - 1], f_s.at[d - 1], f_v.at[d - 1])
            value = value + f_recv[d - 1].astype(F32)

    with jax.named_scope("last"):
        s_send[...] = value
        for j, (dx, dc) in enumerate(others):
            begin(copy(s_send.at[(x + dx) % 2], s_recv.at[j], e_s.at[j], e_v.at[j], at_x(dx, dc)))
        same, other = s_send[xl], None
        for j, (dx, dc) in enumerate(others):
            arrived(s_recv.at[j], e_s.at[j], e_v.at[j])
            if dc == 0:
                same = same + s_recv[j]
            else:
                other = s_recv[j] if other is None else other + s_recv[j]
        hg_out[c] = same
        hg_out[1 - c] = other

    with jax.named_scope("drain"):
        for d in sent:
            d.wait_send()


def body(hidden, weight, labels, cotangent):
    vmem = pl.BlockSpec(memory_space=pltpu.VMEM)
    hbm = pl.BlockSpec(memory_space=pltpu.HBM)
    dma = pltpu.SemaphoreType.DMA
    loss, weight_grad, hg = pl.pallas_call(
        kernel,
        out_shape=(
            jax.ShapeDtypeStruct((1, TOK), F32),
            jax.ShapeDtypeStruct((ROWS, D), BF16),
            jax.ShapeDtypeStruct((2, 16, 256), F32),
        ),
        in_specs=[vmem, hbm, vmem, vmem],
        out_specs=(vmem, vmem, vmem),
        scratch_shapes=[
            pltpu.VMEM((ROWS, D), BF16),
            pltpu.VMEM((SHARDS, 2, 16, PACK), BF16),
            pltpu.VMEM((REST, D), BF16),
            pltpu.VMEM((ROWS, TOK), F32),
            pltpu.VMEM((ROWS, TOK), BF16),
            pltpu.VMEM((8, TOK), F32),
            pltpu.VMEM((3, 1, 1152), F32),
            pltpu.VMEM((21, 1, 1152), F32),
            pltpu.VMEM((2, RING, RING, 2, 16, 256), BF16),
            pltpu.VMEM((RING, RING, 2, 16, 256), BF16),
            pltpu.VMEM((RIGHT, RING, 2, 16, 256), BF16),
            pltpu.VMEM((LEFT, RING, 2, 16, 256), BF16),
            pltpu.VMEM((RIGHT, RING, 2, 16, 256), BF16),
            pltpu.VMEM((LEFT, RING, 2, 16, 256), BF16),
            pltpu.VMEM((RING, 2, 16, 256), F32),
            pltpu.VMEM((RING, 2, 16, 256), BF16),
            pltpu.VMEM((RING - 1, 2, 16, 256), BF16),
            pltpu.VMEM((2, 16, 256), F32),
            pltpu.VMEM((7, 16, 256), F32),
            dma,
            dma((2, RIGHT, 2)), dma((2, RIGHT, 2)),
            dma((RING, 2)), dma((RING, 2)),
            dma((RING, 2, 2)), dma((RING, 2, 2)),
            dma((21,)), dma((21,)),
            dma((RING,)), dma((RING,)),
            dma((2, RIGHT, 2)), dma((2, RIGHT, 2)),
            dma((RING - 1,)), dma((RING - 1,)),
            dma((7,)), dma((7,)),
        ],
        compiler_params=pltpu.CompilerParams(
            collective_id=0, has_side_effects=True, vmem_limit_bytes=51 * 1024 * 1024
        ),
        name="step",
    )(hidden, weight, labels.reshape(1, TOK), cotangent.reshape(1, TOK))

    me = lax.axis_index(DP)
    token_loss = jnp.concatenate([
        lax.dynamic_slice(loss[0], (me * 16,), (16,)),
        lax.dynamic_slice(loss[0], (MAIN + me * 4,), (4,)),
    ])
    block = lax.axis_index("cls_1") * 2 + lax.axis_index("cls_2")
    main = jnp.concatenate([hg[0], hg[1, :, :128]], axis=1)
    main = lax.dynamic_slice(main, (0, block * 96), (16, 96))
    rest = lax.dynamic_slice(hg[1], (block * 4, 128), (4, 96))
    hidden_grad = jnp.concatenate([main, rest], axis=0).astype(BF16)
    return (token_loss, weight_grad, hidden_grad)


def solution(mesh):
    torus = Mesh(mesh.devices.reshape(8, 2, 2, 8, 2), ("cls_0", "cls_1", "cls_2", "dp_0", "dp_1"))
    in_specs = (P(DP, None), P(CLS_DP, None), P(), P())
    out_specs = (P(DP), P(CLS_DP, None), P(DP, CLS))
    return jax.shard_map(body, mesh=torus, in_specs=in_specs, out_specs=out_specs, check_vma=False)
```

time: 86.9 us -> 83.4 us (0.960)
  local copies, waits for them, and re-layouts: 6.98 us -> 3.84 us
    slice x4 -> x0, local copies, waits for them, and re-layouts: 1.86 us -> none  [the longest x1 0.91 us: body(): wide = hidden[:16].reshape(16, 2, HALF).transpose(1, 0, 2)]
    reshape x8 -> x2, local copies, waits for them, and re-layouts: 1.89 us -> 1.37 us  [the longest x1 0.68 us: body(): labels.reshape(1, TOK)]
where the time goes in v2:
time: 83.4 us; the launch traced here: 83.2 us
  Pallas kernels  77.4 us (93%)
  local copies, waits for them, and re-layouts  3.84 us (5%)
  other arithmetic  1.29 us (2%)
    pallas_call x1, Pallas kernels, body(): pl.pallas_call(kernel, out_shape=(jax.ShapeDtypeStruct((1, TOK), F32), ja...  77.4 us
    unnamed x3, local copies, waits for them, and re-layouts  2.31 us

profile of v2, /device:TPU:1, one launch (start us, length us, event | category | flops | bytes accessed | tf_op | source)
XLA Modules:
  0.0 83.2 jit_solution(16272633259998987934)
XLA Ops:
  0.6 0.7 reshape.16.labels
  1.3 0.7 reshape.17.cot
  2.0 0.0 copy-start
  2.0 0.9 %copy-done = bf16[20,3072]{1,0:T(8,128)(2,1)S(1)} copy-done((bf16[20,3072]{1,0:T(8,128)(2,1)S(1)}, bf16[20,3072]{1,0:T(8,128)(2,1)}, u32[]{:S(2)}) %copy-start) | copy-done | bytes 122904
  2.9 77.4 %step.1 = (f32[1,320]{1,0:T(1,128)S(1)}, bf16[384,3072]{1,0:T(8,128)(2,1)S(1)}, f32[2,16,256]{2,1,0:T(8,128)S(1)}) custom-call(bf16[20,3072]{1,0:T(8,128)(2,1)S(1)} %copy-done, bf16[384,3072]{1,0:T(8,128)(2,1)} %w_hbm.1, s32[1,320]{1,0:T(1,128)S(1)} %reshape.16.labels, f32[1,320]{1,0:T(1,128)S(1)} %reshape.17.cot), custom_call_target="tpu_custom_call" | custom-call | tf_op jit(solution)/shard_map/step/pallas_call | solution.py:337
  80.4 0.1 fusion.1
  80.5 0.6 pad_maximum_fusion
  81.1 0.1 fusion.3
  81.2 0.1 fusion.4
  81.2 0.6 pad_maximum_fusion.1
  81.8 1.4 %copy.8 = bf16[384,3072]{1,0:T(8,128)(2,1)} copy(bf16[384,3072]{1,0:T(8,128)(2,1)S(1)} %get-tuple-element.15) | data formatting | bytes 4718592
  (3 shorter events, 0.0 us)
Async XLA Ops:
  2.0 0.9 %copy-start = (bf16[20,3072]{1,0:T(8,128)(2,1)S(1)}, bf16[20,3072]{1,0:T(8,128)(2,1)}, u32[]{:S(2)}) copy-start(bf16[20,3072]{1,0:T(8,128)(2,1)} %hid.1) | copy-start | bytes 368644
